TPU v7x, 64 devices: a 2x2x8 block of a 4x4x8 slice. The times are simulated.
64 devices in a mesh: dp: 4 (over x, y), wg: 16 (over z, core).
Axes of the slice: x: 2, y: 2, z: 8, core: 2. Of those that a mesh axis runs over, the one named last changes fastest.
The devices are a block of a 4x4x8 slice.
Arguments:
- hidden: bfloat16 [65536, 1024], P(('dp', 'wg')), parts along dimension 0
- choice: int32 [65536, 8], P(('dp', 'wg')), parts along dimension 0
- pre_scale: float32 [1024], replicated
- w_router: bfloat16 [1024, 32], replicated
- w_gelu: bfloat16 [32, 1024, 512], P(None, None, 'wg')
- w_linear: bfloat16 [32, 1024, 512], P(None, None, 'wg')
- w_down: bfloat16 [32, 512, 1024], P(None, 'wg')
- post_scale: float32 [1024], replicated
Outputs:
- output: bfloat16 [65536, 1024], P(('dp', 'wg')), parts along dimension 0
There are 4 independent parts. A program takes and returns all parts, laid end to end along the dimension named above; an argument that names none is the same for every part.
All inputs are finite; a program needn't handle non-finite values.
Results may differ from a plain program's by a relative error of at most 0.001.
Values are sent between devices in bfloat16 or wider.
A program may use at most 768 MiB of HBM per device.

v0:
```python
import jax
import jax.numpy as jnp
from jax import lax
from jax.sharding import PartitionSpec as P

EPS = 1e-5


def rms_norm(values, gain_vec):
    return values * lax.rsqrt(jnp.mean(values * values, axis=-1, keepdims=True) + EPS) * gain_vec


def route_slots(block_ids, num_experts, capacity):
    tok_rows, top_k = block_ids.shape
    flat_ids = block_ids.reshape(-1)
    sort_order = jnp.argsort(flat_ids, stable=True)
    counts = jnp.sum((flat_ids[:, None] == jnp.arange(num_experts)[None, :]).astype(jnp.int32), axis=0)
    starts = jnp.cumsum(counts) - counts
    slot_rank = jnp.arange(capacity)
    source = jnp.minimum(starts[:, None] + slot_rank[None, :], tok_rows * top_k - 1)
    slot_token = sort_order[source].reshape(-1) // top_k
    sorted_pos = jnp.argsort(sort_order, stable=True)
    slot_of = flat_ids * capacity + sorted_pos - starts[flat_ids]
    return slot_token, slot_of


def solution(mesh):
    def local_block(hidden, choice, pre_scale, w_router, w_gelu, w_linear, w_down, post_scale):
        tok_rows, d_model = hidden.shape
        num_experts = w_gelu.shape[0]
        top_k = choice.shape[1]
        capacity = 2 * tok_rows * top_k // num_experts
        hidden_f = hidden.astype(jnp.float32)
        normed = rms_norm(hidden_f, pre_scale).astype(jnp.bfloat16)
        router_probs = jax.nn.softmax(jnp.dot(normed, w_router, preferred_element_type=jnp.float32), axis=-1)
        gate_vals = jnp.take_along_axis(router_probs, choice, axis=1)
        slot_token, slot_of = route_slots(choice, num_experts, capacity)
        dispatched = jnp.take(normed, slot_token, axis=0).reshape(num_experts, capacity, d_model)

        def one_expert(expert_args):
            expert_rows, gelu_part, linear_part, down_part = expert_args
            gelu_full = lax.all_gather(gelu_part, 'wg', axis=1, tiled=True)
            linear_full = lax.all_gather(linear_part, 'wg', axis=1, tiled=True)
            down_full = lax.all_gather(down_part, 'wg', axis=0, tiled=True)
            gelu_in = jnp.dot(expert_rows, gelu_full, preferred_element_type=jnp.float32)
            linear_in = jnp.dot(expert_rows, linear_full, preferred_element_type=jnp.float32)
            hidden_act = (jax.nn.gelu(gelu_in, approximate=True) * linear_in).astype(jnp.bfloat16)
            return jnp.dot(hidden_act, down_full, preferred_element_type=jnp.float32)

        expert_out = lax.map(one_expert, (dispatched, w_gelu, w_linear, w_down)).reshape(num_experts * capacity, d_model)
        picked = jnp.take(expert_out, slot_of, axis=0).reshape(tok_rows, top_k, d_model)
        mixed_out = jnp.sum(picked * gate_vals[:, :, None], axis=1)
        return (hidden_f + rms_norm(mixed_out, post_scale)).astype(jnp.bfloat16)

    row_spec = P(('dp', 'wg'), None)
    weight_in = P(None, None, 'wg')
    return jax.shard_map(local_block, mesh=mesh, in_specs=(row_spec, row_spec, P(), P(), weight_in, weight_in, P(None, 'wg', None), P()), out_specs=row_spec, check_vma=False)
```

profile of v0, /device:TPU:21, one launch (start us, length us, event | category | flops | bytes accessed | tf_op | source)
XLA Modules:
  0.0 4071.6 jit_solution(11560918595971234984)
XLA Ops:
  31.6 90.7 %gather_fusion = s32[16384]{0:T(1024)S(1)} fusion(s32[8192]{0:T(1024)S(1)} %get-tuple-element.39, s32[16384]{0:T(1024)S(1)} %broadcast_clamp_fusion.1), kind=kCustom, calls=%fused_computation | custom fusion | bytes 196608 | tf_op jit(solution)/shard_map/gather | solution.py:21
  145.8 65.5 %gather_fusion.3 = f32[8192]{0:T(1024)S(1)} fusion(f32[1024,32]{0,1:T(8,128)S(1)} %fusion.37, s32[8192]{0:T(1024)S(1)} %reshape.307), kind=kCustom, calls=%fused_computation.3 | custom fusion | bytes 131072 | tf_op jit(solution)/shard_map/jit(take_along_axis)/gather | solution.py:36
  212.8 82.1 %gather_fusion.1 = bf16[16384,1024]{1,0:T(8,128)(2,1)} fusion(bf16[1024,1024]{1,0:T(8,128)(2,1)} %copy-done.2, s32[16384]{0:T(1024)S(1)} %copy-done.8), kind=kCustom, calls=%fused_computation.1 | custom fusion | bytes 67174400 | tf_op jit(solution)/shard_map/jit(_take)/gather | solution.py:38
  317.7 3571.4 %while.10 = (s32[]{:T(128)}, f32[32,512,1024]{2,1,0:T(8,128)}, bf16[32,512,1024]{2,1,0:T(8,128)(2,1)}, bf16[32,1024,32]{1,2,0:T(8,128)(2,1)}, bf16[32,1024,32]{1...) while((s32[]{:T(128)}, f32[32,512,1024]{2,1,0:T(8,128)}, bf16[32,512,1024]{2,1,0:T(8,128)(2,1)}, ...), condition=%wide.region_6.7_spmd, body=%wide.region_5.6_spmd.sunk | while | flops 1613234176 | bytes 19858652 | solution.py:50
  322.6 38.0 all-gather.13.cloned.1.call-done
  395.9 35.4 all-gather.17.cloned.1.call-done
  507.2 35.3 all-gather.17.cloned.1.call-done
  618.7 35.4 all-gather.17.cloned.1.call-done
  696.9 33.1 all-gather.15.cloned.1.call-done
  730.1 35.3 all-gather.17.cloned.1.call-done
  841.5 35.3 all-gather.17.cloned.1.call-done
  952.6 35.3 all-gather.17.cloned.1.call-done
  1064.0 35.4 all-gather.17.cloned.1.call-done
  1142.6 33.1 all-gather.15.cloned.1.call-done
  1175.7 35.3 all-gather.17.cloned.1.call-done
  1287.1 35.3 all-gather.17.cloned.1.call-done
  1365.5 33.1 all-gather.15.cloned.1.call-done
  1398.7 35.3 all-gather.17.cloned.1.call-done
  1477.0 33.1 all-gather.15.cloned.1.call-done
  1510.2 35.3 all-gather.17.cloned.1.call-done
  1621.7 35.3 all-gather.17.cloned.1.call-done
  1699.8 33.1 all-gather.15.cloned.1.call-done
  1732.9 35.3 all-gather.17.cloned.1.call-done
  1844.5 35.4 all-gather.17.cloned.1.call-done
  1955.8 35.3 all-gather.17.cloned.1.call-done
  2066.9 35.3 all-gather.17.cloned.1.call-done
  2178.1 35.3 all-gather.17.cloned.1.call-done
  2289.5 35.4 all-gather.17.cloned.1.call-done
  2401.2 35.4 all-gather.17.cloned.1.call-done
  2512.4 35.4 all-gather.17.cloned.1.call-done
  2591.0 33.1 all-gather.15.cloned.1.call-done
  2624.1 35.3 all-gather.17.cloned.1.call-done
  2735.3 35.3 all-gather.17.cloned.1.call-done
  2846.5 35.4 all-gather.17.cloned.1.call-done
  2924.8 33.1 all-gather.15.cloned.1.call-done
  2957.9 35.3 all-gather.17.cloned.1.call-done
  3069.0 35.4 all-gather.17.cloned.1.call-done
  3147.2 33.1 all-gather.15.cloned.1.call-done
  3180.4 35.4 all-gather.17.cloned.1.call-done
  3292.1 35.4 all-gather.17.cloned.1.call-done
  3370.3 33.1 all-gather.15.cloned.1.call-done
  3403.4 35.3 all-gather.17.cloned.1.call-done
  3514.8 35.3 all-gather.17.cloned.1.call-done
  3592.9 33.1 all-gather.15.cloned.1.call-done
  3626.0 35.4 all-gather.17.cloned.1.call-done
  3737.5 35.3 all-gather.17.cloned.1.call-done
  3849.1 35.4 all-gather.17.cloned.1.call-done
  3889.1 153.8 %gather_fusion.2 = f32[8192,1024]{1,0:T(8,128)} fusion(f32[16384,1024]{1,0:T(8,128)} %bitcast.42, s32[8192]{0:T(1024)S(1)} %copy-done.9), kind=kCustom, calls=%fused_computation.2 | custom fusion | bytes 67141632 | tf_op jit(solution)/shard_map/jit(_take)/gather | solution.py:51
  (476 shorter events, 2164.7 us)
Async XLA Ops:
  319.4 76.6 %all-gather.15.cloned.1.call-start = ((), (), s32[]{:S(2)}) async-start(), calls=%async_computation.1 | async-start | bytes 1114112 | tf_op jit(solution)/shard_map/while/body/eval_jaxpr/all_gather | solution.py:44
  321.0 110.4 %all-gather.17.cloned.1.call-start = ((), (), s32[]{:S(2)}) async-start(), calls=%async_computation.2 | async-start | bytes 1114112 | tf_op jit(solution)/shard_map/while/body/eval_jaxpr/all_gather | solution.py:43
  439.2 103.3 %all-gather.17.cloned.1.call-start = ((), (), s32[]{:S(2)}) async-start(), calls=%async_computation.2 | async-start | bytes 1114112 | tf_op jit(solution)/shard_map/while/body/eval_jaxpr/all_gather | solution.py:43
  548.6 70.1 %all-gather.15.cloned.1.call-start = ((), (), s32[]{:S(2)}) async-start(), calls=%async_computation.1 | async-start | bytes 1114112 | tf_op jit(solution)/shard_map/while/body/eval_jaxpr/all_gather | solution.py:44
  550.2 103.9 %all-gather.17.cloned.1.call-start = ((), (), s32[]{:S(2)}) async-start(), calls=%async_computation.2 | async-start | bytes 1114112 | tf_op jit(solution)/shard_map/while/body/eval_jaxpr/all_gather | solution.py:43
  661.9 103.4 %all-gather.17.cloned.1.call-start = ((), (), s32[]{:S(2)}) async-start(), calls=%async_computation.2 | async-start | bytes 1114112 | tf_op jit(solution)/shard_map/while/body/eval_jaxpr/all_gather | solution.py:43
  771.5 69.9 %all-gather.15.cloned.1.call-start = ((), (), s32[]{:S(2)}) async-start(), calls=%async_computation.1 | async-start | bytes 1114112 | tf_op jit(solution)/shard_map/while/body/eval_jaxpr/all_gather | solution.py:44
  773.1 103.6 %all-gather.17.cloned.1.call-start = ((), (), s32[]{:S(2)}) async-start(), calls=%async_computation.2 | async-start | bytes 1114112 | tf_op jit(solution)/shard_map/while/body/eval_jaxpr/all_gather | solution.py:43
  884.6 103.3 %all-gather.17.cloned.1.call-start = ((), (), s32[]{:S(2)}) async-start(), calls=%async_computation.2 | async-start | bytes 1114112 | tf_op jit(solution)/shard_map/while/body/eval_jaxpr/all_gather | solution.py:43
  994.0 69.9 %all-gather.15.cloned.1.call-start = ((), (), s32[]{:S(2)}) async-start(), calls=%async_computation.1 | async-start | bytes 1114112 | tf_op jit(solution)/shard_map/while/body/eval_jaxpr/all_gather | solution.py:44
  995.6 103.8 %all-gather.17.cloned.1.call-start = ((), (), s32[]{:S(2)}) async-start(), calls=%async_computation.2 | async-start | bytes 1114112 | tf_op jit(solution)/shard_map/while/body/eval_jaxpr/all_gather | solution.py:43
  1105.6 70.1 %all-gather.15.cloned.1.call-start = ((), (), s32[]{:S(2)}) async-start(), calls=%async_computation.1 | async-start | bytes 1114112 | tf_op jit(solution)/shard_map/while/body/eval_jaxpr/all_gather | solution.py:44
  1107.2 103.8 %all-gather.17.cloned.1.call-start = ((), (), s32[]{:S(2)}) async-start(), calls=%async_computation.2 | async-start | bytes 1114112 | tf_op jit(solution)/shard_map/while/body/eval_jaxpr/all_gather | solution.py:43
  1217.2 69.9 %all-gather.15.cloned.1.call-start = ((), (), s32[]{:S(2)}) async-start(), calls=%async_computation.1 | async-start | bytes 1114112 | tf_op jit(solution)/shard_map/while/body/eval_jaxpr/all_gather | solution.py:44
  1218.8 103.6 %all-gather.17.cloned.1.call-start = ((), (), s32[]{:S(2)}) async-start(), calls=%async_computation.2 | async-start | bytes 1114112 | tf_op jit(solution)/shard_map/while/body/eval_jaxpr/all_gather | solution.py:43
  1328.6 70.1 %all-gather.15.cloned.1.call-start = ((), (), s32[]{:S(2)}) async-start(), calls=%async_computation.1 | async-start | bytes 1114112 | tf_op jit(solution)/shard_map/while/body/eval_jaxpr/all_gather | solution.py:44
  1330.2 103.8 %all-gather.17.cloned.1.call-start = ((), (), s32[]{:S(2)}) async-start(), calls=%async_computation.2 | async-start | bytes 1114112 | tf_op jit(solution)/shard_map/while/body/eval_jaxpr/all_gather | solution.py:43
  1440.1 70.1 %all-gather.15.cloned.1.call-start = ((), (), s32[]{:S(2)}) async-start(), calls=%async_computation.1 | async-start | bytes 1114112 | tf_op jit(solution)/shard_map/while/body/eval_jaxpr/all_gather | solution.py:44
  1441.7 103.7 %all-gather.17.cloned.1.call-start = ((), (), s32[]{:S(2)}) async-start(), calls=%async_computation.2 | async-start | bytes 1114112 | tf_op jit(solution)/shard_map/while/body/eval_jaxpr/all_gather | solution.py:43
  1551.6 70.1 %all-gather.15.cloned.1.call-start = ((), (), s32[]{:S(2)}) async-start(), calls=%async_computation.1 | async-start | bytes 1114112 | tf_op jit(solution)/shard_map/while/body/eval_jaxpr/all_gather | solution.py:44
  1553.2 103.7 %all-gather.17.cloned.1.call-start = ((), (), s32[]{:S(2)}) async-start(), calls=%async_computation.2 | async-start | bytes 1114112 | tf_op jit(solution)/shard_map/while/body/eval_jaxpr/all_gather | solution.py:43
  1664.7 103.4 %all-gather.17.cloned.1.call-start = ((), (), s32[]{:S(2)}) async-start(), calls=%async_computation.2 | async-start | bytes 1114112 | tf_op jit(solution)/shard_map/while/body/eval_jaxpr/all_gather | solution.py:43
  1774.4 70.1 %all-gather.15.cloned.1.call-start = ((), (), s32[]{:S(2)}) async-start(), calls=%async_computation.1 | async-start | bytes 1114112 | tf_op jit(solution)/shard_map/while/body/eval_jaxpr/all_gather | solution.py:44
  1776.0 103.9 %all-gather.17.cloned.1.call-start = ((), (), s32[]{:S(2)}) async-start(), calls=%async_computation.2 | async-start | bytes 1114112 | tf_op jit(solution)/shard_map/while/body/eval_jaxpr/all_gather | solution.py:43
  1887.7 103.4 %all-gather.17.cloned.1.call-start = ((), (), s32[]{:S(2)}) async-start(), calls=%async_computation.2 | async-start | bytes 1114112 | tf_op jit(solution)/shard_map/while/body/eval_jaxpr/all_gather | solution.py:43
  1998.9 103.3 %all-gather.17.cloned.1.call-start = ((), (), s32[]{:S(2)}) async-start(), calls=%async_computation.2 | async-start | bytes 1114112 | tf_op jit(solution)/shard_map/while/body/eval_jaxpr/all_gather | solution.py:43
  2110.0 103.4 %all-gather.17.cloned.1.call-start = ((), (), s32[]{:S(2)}) async-start(), calls=%async_computation.2 | async-start | bytes 1114112 | tf_op jit(solution)/shard_map/while/body/eval_jaxpr/all_gather | solution.py:43
  2221.2 103.7 %all-gather.17.cloned.1.call-start = ((), (), s32[]{:S(2)}) async-start(), calls=%async_computation.2 | async-start | bytes 1114112 | tf_op jit(solution)/shard_map/while/body/eval_jaxpr/all_gather | solution.py:43
  2331.2 70.1 %all-gather.15.cloned.1.call-start = ((), (), s32[]{:S(2)}) async-start(), calls=%async_computation.1 | async-start | bytes 1114112 | tf_op jit(solution)/shard_map/while/body/eval_jaxpr/all_gather | solution.py:44
  2332.8 103.9 %all-gather.17.cloned.1.call-start = ((), (), s32[]{:S(2)}) async-start(), calls=%async_computation.2 | async-start | bytes 1114112 | tf_op jit(solution)/shard_map/while/body/eval_jaxpr/all_gather | solution.py:43
  2444.4 103.4 %all-gather.17.cloned.1.call-start = ((), (), s32[]{:S(2)}) async-start(), calls=%async_computation.2 | async-start | bytes 1114112 | tf_op jit(solution)/shard_map/while/body/eval_jaxpr/all_gather | solution.py:43
  2554.0 70.1 %all-gather.15.cloned.1.call-start = ((), (), s32[]{:S(2)}) async-start(), calls=%async_computation.1 | async-start | bytes 1114112 | tf_op jit(solution)/shard_map/while/body/eval_jaxpr/all_gather | solution.py:44
  2555.6 103.8 %all-gather.17.cloned.1.call-start = ((), (), s32[]{:S(2)}) async-start(), calls=%async_computation.2 | async-start | bytes 1114112 | tf_op jit(solution)/shard_map/while/body/eval_jaxpr/all_gather | solution.py:43
  2667.2 103.4 %all-gather.17.cloned.1.call-start = ((), (), s32[]{:S(2)}) async-start(), calls=%async_computation.2 | async-start | bytes 1114112 | tf_op jit(solution)/shard_map/while/body/eval_jaxpr/all_gather | solution.py:43
  2778.4 103.6 %all-gather.17.cloned.1.call-start = ((), (), s32[]{:S(2)}) async-start(), calls=%async_computation.2 | async-start | bytes 1114112 | tf_op jit(solution)/shard_map/while/body/eval_jaxpr/all_gather | solution.py:43
  2889.8 103.4 %all-gather.17.cloned.1.call-start = ((), (), s32[]{:S(2)}) async-start(), calls=%async_computation.2 | async-start | bytes 1114112 | tf_op jit(solution)/shard_map/while/body/eval_jaxpr/all_gather | solution.py:43
  3001.0 103.4 %all-gather.17.cloned.1.call-start = ((), (), s32[]{:S(2)}) async-start(), calls=%async_computation.2 | async-start | bytes 1114112 | tf_op jit(solution)/shard_map/while/body/eval_jaxpr/all_gather | solution.py:43
  3112.2 103.6 %all-gather.17.cloned.1.call-start = ((), (), s32[]{:S(2)}) async-start(), calls=%async_computation.2 | async-start | bytes 1114112 | tf_op jit(solution)/shard_map/while/body/eval_jaxpr/all_gather | solution.py:43
  3222.0 70.1 %all-gather.15.cloned.1.call-start = ((), (), s32[]{:S(2)}) async-start(), calls=%async_computation.1 | async-start | bytes 1114112 | tf_op jit(solution)/shard_map/while/body/eval_jaxpr/all_gather | solution.py:44
  3223.6 103.9 %all-gather.17.cloned.1.call-start = ((), (), s32[]{:S(2)}) async-start(), calls=%async_computation.2 | async-start | bytes 1114112 | tf_op jit(solution)/shard_map/while/body/eval_jaxpr/all_gather | solution.py:43
  3335.2 103.4 %all-gather.17.cloned.1.call-start = ((), (), s32[]{:S(2)}) async-start(), calls=%async_computation.2 | async-start | bytes 1114112 | tf_op jit(solution)/shard_map/while/body/eval_jaxpr/all_gather | solution.py:43
  3444.8 69.9 %all-gather.15.cloned.1.call-start = ((), (), s32[]{:S(2)}) async-start(), calls=%async_computation.1 | async-start | bytes 1114112 | tf_op jit(solution)/shard_map/while/body/eval_jaxpr/all_gather | solution.py:44
  3446.4 103.6 %all-gather.17.cloned.1.call-start = ((), (), s32[]{:S(2)}) async-start(), calls=%async_computation.2 | async-start | bytes 1114112 | tf_op jit(solution)/shard_map/while/body/eval_jaxpr/all_gather | solution.py:43
  3557.8 103.6 %all-gather.17.cloned.1.call-start = ((), (), s32[]{:S(2)}) async-start(), calls=%async_computation.2 | async-start | bytes 1114112 | tf_op jit(solution)/shard_map/while/body/eval_jaxpr/all_gather | solution.py:43
  3667.6 69.9 %all-gather.15.cloned.1.call-start = ((), (), s32[]{:S(2)}) async-start(), calls=%async_computation.1 | async-start | bytes 1114112 | tf_op jit(solution)/shard_map/while/body/eval_jaxpr/all_gather | solution.py:44
  3669.2 103.6 %all-gather.17.cloned.1.call-start = ((), (), s32[]{:S(2)}) async-start(), calls=%async_computation.2 | async-start | bytes 1114112 | tf_op jit(solution)/shard_map/while/body/eval_jaxpr/all_gather | solution.py:43
  3779.0 70.1 %all-gather.15.cloned.1.call-start = ((), (), s32[]{:S(2)}) async-start(), calls=%async_computation.1 | async-start | bytes 1114112 | tf_op jit(solution)/shard_map/while/body/eval_jaxpr/all_gather | solution.py:44
  3780.6 103.9 %all-gather.17.cloned.1.call-start = ((), (), s32[]{:S(2)}) async-start(), calls=%async_computation.2 | async-start | bytes 1114112 | tf_op jit(solution)/shard_map/while/body/eval_jaxpr/all_gather | solution.py:43
  (61 other events, 6740.7 us)
Sparse Core Ops, SparseCore 0:
  320.2 40.2 all-gather.12
  362.2 33.7 all-gather.14
  397.6 33.7 all-gather.16
  438.1 33.7 all-gather.12
  508.7 33.7 all-gather.16
  549.5 33.7 all-gather.12
  584.9 33.7 all-gather.14
  620.3 33.7 all-gather.16
  696.3 33.7 all-gather.14
  731.6 33.7 all-gather.16
  772.4 33.7 all-gather.12
  843.0 33.7 all-gather.16
  918.8 33.7 all-gather.14
  954.1 33.7 all-gather.16
  994.9 33.7 all-gather.12
  1065.6 33.7 all-gather.16
  1106.5 33.7 all-gather.12
  1141.9 33.7 all-gather.14
  1177.2 33.7 all-gather.16
  1218.0 33.7 all-gather.12
  1253.3 33.7 all-gather.14
  1329.5 33.7 all-gather.12
  1552.5 33.7 all-gather.12
  1623.2 33.7 all-gather.16
  1699.1 33.7 all-gather.14
  1775.3 33.7 all-gather.12
  1846.1 33.7 all-gather.16
  1886.6 33.7 all-gather.12
  2109.0 33.7 all-gather.12
  2220.5 33.7 all-gather.12
  2332.0 33.7 all-gather.12
  2402.9 33.7 all-gather.16
  2478.7 33.7 all-gather.14
  2514.1 33.7 all-gather.16
  2590.3 33.7 all-gather.14
  2666.2 33.7 all-gather.12
  2777.3 33.7 all-gather.12
  2848.2 33.7 all-gather.16
  2924.2 33.7 all-gather.14
  2999.9 33.7 all-gather.12
  3111.1 33.7 all-gather.12
  3293.7 33.7 all-gather.16
  3369.6 33.7 all-gather.14
  3445.7 33.7 all-gather.12
  3556.8 33.7 all-gather.12
  3592.2 33.7 all-gather.14
  3739.0 33.7 all-gather.16
  3815.3 33.7 all-gather.14
  (48 shorter events, 1616.9 us)
where the time goes:
time: 4080 us; the launch traced here: 4070 us
  waiting for transfers between devices  3200 us (78%)
  local copies, waits for them, and re-layouts  541 us (13%)
  matrix products  222 us (5%)
  other arithmetic  86.2 us (2%)
    all_gather x32, waiting for transfers between devices, one_expert(): linear_full = lax.all_gather(linear_part, 'wg', axis=1, tiled=True)  1130 us
    all_gather x32, waiting for transfers between devices, one_expert(): down_full = lax.all_gather(down_part, 'wg', axis=0, tiled=True)  1060 us
    all_gather x32, waiting for transfers between devices, one_expert(): gelu_full = lax.all_gather(gelu_part, 'wg', axis=1, tiled=True)  1010 us
    gather x1, local copies, waits for them, and re-layouts, local_block(): jnp.take(expert_out, slot_of, axis=0).reshape(tok_rows, top_k, d_model)  154 us
    dot_general x32, matrix products, one_expert(): return jnp.dot(hidden_act, down_full, preferred_element_type=jnp.float32)  149 us
    dynamic_slice x96, local copies, waits for them, and re-layouts, local_block(): lax.map(one_expert, (dispatched, w_gelu, w_linear, w_down))  141 us
    gather x2, local copies, waits for them, and re-layouts, route_slots(): slot_token = sort_order[source].reshape(-1) // top_k  90.7 us
    gather x1, local copies, waits for them, and re-layouts, local_block(): jnp.take(normed, slot_token, axis=0).reshape(num_experts, capacity, d_model)  82.1 us
  transfers between devices with their start and end apart: 96, of which 96 were waited for; matrix products, arithmetic and copies ran while one was open for 4% of the time, Pallas kernels for 0%

commit v1 on v0

v1 whole, which is shorter than its diff:
```python
import functools
import math

import jax
import jax.numpy as jnp
from jax import lax
from jax.experimental import pallas as pl
from jax.experimental.pallas import tpu as pltpu
from jax.sharding import PartitionSpec as P

EPS = 1e-5
MESH = pl.DeviceIdType.MESH
VMEM_BYTES = 67_043_328


def dot_t(lhs, rhs):
    return lax.dot_general(lhs, rhs, (((1,), (1,)), ((), ())), preferred_element_type=jnp.float32)


def moe_kernel(side, chips, blk, hid_ref, choice_ref, pre_ref, router_ref, wg_ref, wl_ref, wd_ref, own_out, part_out,
               wts, rows, acc, gates, up_ss, up_rs, dn_ss, dn_rs, x_ss, x_rs, y_ss, y_rs, load_sem, sib_ss, sib_rs, part_ss, part_rs):
    tok, d_model = hid_ref.shape
    experts, _, _, shard, _ = wts.shape
    width = chips * shard
    rounds = experts // 4
    far = chips // 2
    near = chips - 1 - far
    slots = chips - 1
    nblk = tok // blk
    ncol = min(256, d_model)

    dp, wg = lax.axis_index('dp'), lax.axis_index('wg')
    z, core = wg // 2, wg % 2
    sib = wg + 1 - 2 * core
    up = ((z + 1) % chips) * 2 + core
    down = ((z + chips - 1) % chips) * 2 + core
    gx, gy = dp // side, dp % side
    xdp = dp + side * (1 - 2 * (gx % 2))
    ydp = dp + 1 - 2 * (gy % 2)
    par = (gx + gy) % 2

    def remote(ref, ss, rs, where, h, s):
        return pltpu.make_async_remote_copy(src_ref=ref, dst_ref=ref, send_sem=ss.at[h, s - 1], recv_sem=rs.at[h, s - 1],
                                            device_id=where, device_id_type=MESH)

    def mine(h):
        return 2 * h + par

    def theirs(h):
        return 2 * h + 1 - par

    def behind(s):
        return (z - s + chips) % chips

    def ahead(s):
        return (z + s) % chips

    def up_send(h, s):
        return remote(wts.at[mine(h), behind(s - 1)], up_ss, up_rs, (dp, up), h, s)

    def up_recv(h, s):
        return remote(wts.at[mine(h), behind(s)], up_ss, up_rs, (dp, up), h, s)

    def dn_send(h, s):
        return remote(wts.at[mine(h), ahead(s - 1)], dn_ss, dn_rs, (dp, down), h, s)

    def dn_recv(h, s):
        return remote(wts.at[mine(h), ahead(s)], dn_ss, dn_rs, (dp, down), h, s)

    def x_send(h, s):
        return remote(wts.at[mine(h), behind(s)], x_ss, x_rs, (xdp, wg), h, s)

    def x_recv(h, s):
        return remote(wts.at[theirs(h), behind(s)], x_ss, x_rs, (xdp, wg), h, s)

    def y_send(h, s):
        return remote(wts.at[mine(h), ahead(s)], y_ss, y_rs, (ydp, wg), h, s)

    def y_recv(h, s):
        return remote(wts.at[theirs(h), ahead(s)], y_ss, y_rs, (ydp, wg), h, s)

    def sibling(src, dst, k):
        return pltpu.make_async_remote_copy(src_ref=src, dst_ref=dst, send_sem=sib_ss.at[k], recv_sem=sib_rs.at[k],
                                            device_id=(dp, sib), device_id_type=MESH)

    def partial_sum(c):
        return pltpu.make_async_remote_copy(src_ref=acc.at[1, pl.ds(c * blk, blk)], dst_ref=part_out.at[pl.ds(c * blk, blk)],
                                            send_sem=part_ss.at[c], recv_sem=part_rs.at[c], device_id=(dp, sib), device_id_type=MESH)

    loads = []
    for k, src in enumerate((wg_ref, wl_ref, wd_ref)):
        loads.append(pltpu.make_async_copy(src.at[pl.ds(0, 4)], wts.at[pl.ds(0, 4), z, k], load_sem.at[k]))
    for k, src in enumerate((wg_ref, wl_ref, wd_ref)):
        loads.append(pltpu.make_async_copy(src.at[pl.ds(4, experts - 4)], wts.at[pl.ds(4, experts - 4), z, k], load_sem.at[3 + k]))
    loads.append(pltpu.make_async_copy(hid_ref, rows.at[0], load_sem.at[6]))
    for load in loads:
        load.start()

    barrier = pltpu.get_barrier_semaphore()
    for peer in ((dp, up), (dp, down), (xdp, wg), (ydp, wg), (dp, sib)):
        pl.semaphore_signal(barrier, inc=1, device_id=peer, device_id_type=MESH)
    pl.semaphore_wait(barrier, 5)

    for load in loads[:3]:
        load.wait()
    up_send(0, 1).start()
    dn_send(1, 1).start()
    up_send(1, 1).start()
    dn_send(0, 1).start()

    loads[6].wait()
    nrm = min(128, tok)

    @pl.loop(0, tok // nrm)
    def _(i):
        at = pl.ds(pl.multiple_of(i * nrm, nrm), nrm)
        values = rows[0, at, :].astype(jnp.float32)
        scale = lax.rsqrt(jnp.mean(values * values, axis=-1, keepdims=True) + EPS)
        rows[0, at, :] = (values * scale * pre_ref[...]).astype(jnp.bfloat16)

    for load in loads[3:6]:
        load.wait()

    rtr = min(256, tok)

    @pl.loop(0, tok // rtr)
    def _(i):
        at = pl.ds(pl.multiple_of(i * rtr, rtr), rtr)
        logits = dot_t(router_ref[...], rows[0, at, :])
        shifted = jnp.exp(logits - jnp.max(logits, axis=0, keepdims=True))
        probs = shifted / jnp.sum(shifted, axis=0, keepdims=True)
        expert_ids = lax.broadcasted_iota(jnp.int32, (experts, rtr), 0)
        picks = choice_ref[:, at]
        chosen = expert_ids == picks[0:1, :]
        for j in range(1, picks.shape[0]):
            chosen = chosen | (expert_ids == picks[j:j + 1, :])
        gates[0, at, :] = jnp.where(chosen, probs, -1.0).T

    @pl.loop(0, 2 * tok // nrm)
    def _(i):
        at = pl.ds(pl.multiple_of((i // 2) * nrm, nrm), nrm)
        acc[i % 2, at, :] = jnp.zeros((nrm, d_model), jnp.float32)

    rows_copy = sibling(rows.at[0], rows.at[1], 0)
    gates_copy = sibling(gates.at[0], gates.at[1], 1)
    rows_copy.start()
    gates_copy.start()

    def exchange(r, j, more):
        even, odd = 2 * r, 2 * r + 1
        s = j // 2 + 1
        h_up, n_up = (even, far) if j % 2 == 0 else (odd, near)
        h_dn, n_dn = (odd, far) if j % 2 == 0 else (even, near)
        up_recv(h_up, s).wait_recv()
        if s < n_up:
            up_send(h_up, s + 1).start()
        elif more is not None:
            more(lambda: up_send(even + 2 if j == slots - 2 else odd + 2, 1).start())
        x_send(h_up, s).start()
        dn_recv(h_dn, s).wait_recv()
        if s < n_dn:
            dn_send(h_dn, s + 1).start()
        elif more is not None:
            more(lambda: dn_send(odd + 2 if j == slots - 2 else even + 2, 1).start())
        y_send(h_dn, s).start()

    def arrived(r):
        for h, n_up, n_dn in ((2 * r, far, near), (2 * r + 1, near, far)):
            for s in range(1, n_up + 1):
                x_recv(h, s).wait_recv()
            for s in range(1, n_dn + 1):
                y_recv(h, s).wait_recv()

    def work(r, q):
        odd = q % 2
        rb = (q // 2) % nblk
        half = 1 - (q // (2 * nblk)) % 2
        other = q // (4 * nblk)
        e = 4 * r + 2 * odd + par + other * (1 - 2 * par)
        at = pl.ds(pl.multiple_of(rb * blk, blk), blk)
        x = rows[half, at, :]
        lane = lax.broadcasted_iota(jnp.int32, (blk, experts), 1)
        gate = jnp.sum(jnp.where(lane == e, gates[half, at, :], 0.0), axis=1, keepdims=True)
        u = dot_t(x, wts[e, :, 0].reshape(width, d_model))
        v = dot_t(x, wts[e, :, 1].reshape(width, d_model))
        c = math.sqrt(2.0 / math.pi)
        cdf = 0.5 * (1.0 + jnp.tanh(c * (u + 0.044715 * (u * u * u))))
        a = jnp.where(gate >= 0.0, u * cdf * v, 0.0).astype(jnp.bfloat16)
        for n in range(d_model // ncol):
            cols = pl.ds(n * ncol, ncol)
            o = jnp.dot(a, wts[e, :, 2, :, cols].reshape(width, ncol), preferred_element_type=jnp.float32)
            acc[half, at, cols] += gate * o

    total = 8 * nblk
    cuts = [(total * j + slots - 1) // slots for j in range(slots + 1)]

    for j in range(slots):
        exchange(0, j, (lambda f: f()) if rounds > 1 else None)
    rows_copy.wait_recv()
    gates_copy.wait_recv()

    @pl.loop(1, rounds)
    def _(r):
        waited = False
        for j in range(slots):
            exchange(r, j, lambda f: pl.when(r < rounds - 1)(f))
            if not waited and cuts[j + 1] > total // 2:
                arrived(r - 1)
                waited = True

            @pl.loop(cuts[j], cuts[j + 1])
            def _(q):
                work(r - 1, q)

    last = rounds - 1

    @pl.loop(0, total // 2)
    def _(q):
        work(last, q)

    arrived(last)

    @pl.loop(total // 2, 3 * total // 4)
    def _(q):
        work(last, q)

    for c in range(nblk):
        partial_sum(c).start()

    @pl.loop(3 * total // 4, total)
    def _(q):
        work(last, q)

    own = pltpu.make_async_copy(acc.at[0], own_out, load_sem.at[6])
    own.start()

    @pl.loop(0, rounds)
    def _(r):
        for h, n_up, n_dn in ((2 * r, far, near), (2 * r + 1, near, far)):
            for s in range(1, n_up + 1):
                up_send(h, s).wait_send()
                x_send(h, s).wait_send()
            for s in range(1, n_dn + 1):
                dn_send(h, s).wait_send()
                y_send(h, s).wait_send()

    rows_copy.wait_send()
    gates_copy.wait_send()
    for c in range(nblk):
        partial_sum(c).wait()
    own.wait()


def solution(mesh):
    side = math.isqrt(mesh.shape['dp'])
    chips = mesh.shape['wg'] // 2

    def local_block(hidden, choice, pre_scale, w_router, w_gelu, w_linear, w_down, post_scale):
        tok, d_model = hidden.shape
        experts, _, shard = w_gelu.shape
        blk = min(512, tok // 2)
        half_rounds = experts // 2
        steps = chips // 2
        flow = [pltpu.SemaphoreType.DMA((half_rounds, steps)) for _ in range(8)]
        flops = 2 * 2 * tok * experts * 3 * (chips * shard) * d_model
        own, part = pl.pallas_call(
            functools.partial(moe_kernel, side, chips, blk),
            out_shape=(jax.ShapeDtypeStruct((tok, d_model), jnp.float32), jax.ShapeDtypeStruct((tok, d_model), jnp.float32)),
            in_specs=[
                pl.BlockSpec(memory_space=pl.ANY),
                pl.BlockSpec(memory_space=pltpu.VMEM),
                pl.BlockSpec(memory_space=pltpu.VMEM),
                pl.BlockSpec(memory_space=pltpu.VMEM),
                pl.BlockSpec(memory_space=pl.ANY),
                pl.BlockSpec(memory_space=pl.ANY),
                pl.BlockSpec(memory_space=pl.ANY),
            ],
            out_specs=(pl.BlockSpec(memory_space=pl.ANY), pl.BlockSpec(memory_space=pl.ANY)),
            scratch_shapes=[
                pltpu.VMEM((experts, chips, 3, shard, d_model), jnp.bfloat16),
                pltpu.VMEM((2, tok, d_model), jnp.bfloat16),
                pltpu.VMEM((2, tok, d_model), jnp.float32),
                pltpu.VMEM((2, tok, experts), jnp.float32),
                *flow,
                pltpu.SemaphoreType.DMA((7,)),
                pltpu.SemaphoreType.DMA((2,)),
                pltpu.SemaphoreType.DMA((2,)),
                pltpu.SemaphoreType.DMA((tok // blk,)),
                pltpu.SemaphoreType.DMA((tok // blk,)),
            ],
            compiler_params=pltpu.CompilerParams(collective_id=0, has_side_effects=True, vmem_limit_bytes=VMEM_BYTES),
            cost_estimate=pl.CostEstimate(flops=flops, bytes_accessed=8 * experts * chips * shard * d_model, transcendentals=0),
        )(hidden, choice.T, pre_scale.reshape(1, d_model), w_router.T, jnp.swapaxes(w_gelu, 1, 2), jnp.swapaxes(w_linear, 1, 2), w_down)
        mixed = own + part
        scaled = mixed * lax.rsqrt(jnp.mean(mixed * mixed, axis=-1, keepdims=True) + EPS) * post_scale
        return (hidden.astype(jnp.float32) + scaled).astype(jnp.bfloat16)

    row_spec = P(('dp', 'wg'), None)
    weight_in = P(None, None, 'wg')
    return jax.shard_map(local_block, mesh=mesh, in_specs=(row_spec, row_spec, P(), P(), weight_in, weight_in, P(None, 'wg', None), P()), out_specs=row_spec, check_vma=False)
```

time: 4080 us -> 281 us (0.07)
  waiting for transfers between devices: 3200 us -> 0 us
  local copies, waits for them, and re-layouts: 541 us -> 0.01 us
  Pallas kernels: 0 us -> 275 us
  matrix products: 222 us -> 0 us
  other arithmetic: 86.2 us -> 6.14 us
    all_gather x96 -> x0, waiting for transfers between devices: 3200 us -> none  [the longest x32 1130 us: one_expert(): linear_full = lax.all_gather(linear_part, 'wg', axis=1, tiled=True)]
    gather x11 -> x0, local copies, waits for them, and re-layouts: 395 us -> none  [the longest x1 154 us: local_block(): jnp.take(expert_out, slot_of, axis=0).reshape(tok_rows, top_k, d_model)]
    pallas_call x0 -> x1, Pallas kernels: none -> 275 us  [local_block(): pl.pallas_call(functools.partial(moe_kernel, side, chips, blk), out_shape...]
    dot_general x65 -> x0, matrix products: 222 us -> none  [the longest x32 149 us: one_expert(): return jnp.dot(hidden_act, down_full, preferred_element_type=jnp.float32)]
    dynamic_slice x96 -> x0, local copies, waits for them, and re-layouts: 141 us -> none  [local_block(): lax.map(one_expert, (dispatched, w_gelu, w_linear, w_down))]
  transfers between devices with their start and end apart: 96 -> 0, of which waited for: 96 -> 0; matrix products, arithmetic and copies ran while one was open for 4% -> 0% of each run, Pallas kernels for 0% -> 0%
where the time goes in v1:
time: 281 us
  Pallas kernels  275 us (98%)
  other arithmetic  6.14 us (2%)
    pallas_call x1, Pallas kernels, local_block(): pl.pallas_call(functools.partial(moe_kernel, side, chips, blk), out_shape...  275 us

profile of v1, /device:TPU:21, one launch (start us, length us, event | category | flops | bytes accessed | tf_op | source)
XLA Modules:
  0.0 280.9 jit_solution(13934316298413905130)
XLA Ops:
  0.0 274.7 %shard_map.82 = (f32[1024,1024]{1,0:T(8,128)}, f32[1024,1024]{1,0:T(8,128)}) custom-call(bf16[1024,1024]{1,0:T(8,128)(2,1)} %hid_ref.1, s32[8,1024]{1,0:T(8,128)} %bitcast.8, f32[1,1024]{1,0:T(1,128)} %bitcast.9, bf16[32,1024]{1,0:T(8,128)(2,1)} %bitcast.7, bf16[32,32,1024]{2,1,0:T(8,128)(2,1)} %bitcast.5, bf16[32,32,1024]{2,1,0:T(8,128)(2,1)} %bitcast.6, ...), custom_call_target="tpu_custom_call" | custom-call | flops 103079215104 | bytes 67108864 | tf_op jit(solution)/shard_map/pallas_call | solution.py:266
  274.7 0.0 copy-start
  274.7 0.0 copy-start.1
  274.7 4.1 %multiply_reduce_fusion = (f32[1024]{0:T(1024)S(1)}, f32[1024,1024]{1,0:T(8,128)S(1)}) fusion(f32[1024,1024]{1,0:T(8,128)} %get-tuple-element.7, f32[1024,1024]{1,0:T(8,128)} %get-tuple-element.8), kind=kLoop, calls=%fused_computation.1 | loop fusion | flops 3144704 | bytes 12587008 | tf_op jit(solution)/shard_map/reduce_sum | solution.py:295
  278.9 0.0 copy-done
  278.9 0.0 copy-done.1
  278.9 2.0 add_convert_fusion
  (1 shorter events, 0.0 us)
Async XLA Ops:
  274.7 4.2 %copy-start = (bf16[1024,1024]{1,0:T(8,128)(2,1)S(1)}, bf16[1024,1024]{1,0:T(8,128)(2,1)}, u32[]{:S(2)}) copy-start(bf16[1024,1024]{1,0:T(8,128)(2,1)} %hid_ref.1) | copy-start | bytes 6291460
  274.7 4.2 %copy-start.1 = (f32[1024]{0:T(1024)S(1)}, f32[1024]{0:T(1024)}, u32[]{:S(2)}) copy-start(f32[1024]{0:T(1024)} %param.15) | copy-start | bytes 12292

commit v2 on v0

v2 whole, which is shorter than its diff:
```python
import functools
import math

import jax
import jax.numpy as jnp
from jax import lax
from jax.experimental import pallas as pl
from jax.experimental.pallas import tpu as pltpu
from jax.sharding import PartitionSpec as P

EPS = 1e-5
MESH = pl.DeviceIdType.MESH
VMEM_BYTES = 67_043_328


def dot_t(lhs, rhs):
    return lax.dot_general(lhs, rhs, (((1,), (1,)), ((), ())), preferred_element_type=jnp.float32)


def exclusive_experts(experts):
    count = experts * 11 // 32
    while (experts - count) % 3:
        count -= 1
    return count


def moe_kernel(side, chips, blk, excl, hid_ref, choice_ref, pre_ref, router_ref, wg_ref, wl_ref, wd_ref, own_out, part_out, cross_out, fold_out,
               wts, rows, acc, gate_t, gates, tmp, up_ss, up_rs, dn_ss, dn_rs, y_ss, y_rs, load_sem, row_ss, row_rs, gate_ss, gate_rs,
               fold_ss, fold_rs, cross_ss, cross_rs, part_ss, part_rs):
    tok, d_model = hid_ref.shape
    held, _, _, shard, _ = wts.shape
    experts = held + excl
    width = chips * shard
    slots = chips - 1
    rounds = held // 3
    count = rounds * slots
    nblk = tok // blk
    ncol = min(256, d_model)

    dp, wg = lax.axis_index('dp'), lax.axis_index('wg')
    z, core = wg // 2, wg % 2
    gx, gy = dp // side, dp % side
    px, py = gx % 2, gy % 2
    up = (dp, ((z + 1) % chips) * 2 + core)
    down = (dp, ((z + chips - 1) % chips) * 2 + core)
    sib = (dp, wg + 1 - 2 * core)
    cross = (dp + side * (1 - 2 * px), wg)
    along = (dp + 1 - 2 * py, wg)

    def remote(src, dst, ss, rs, where):
        return pltpu.make_async_remote_copy(src_ref=src, dst_ref=dst, send_sem=ss, recv_sem=rs, device_id=where, device_id_type=MESH)

    def mine(r):
        return 3 * r + 2 * py

    def slice_copy(i, chip, ss, rs, m, where):
        ref = wts.at[i, chip]
        return remote(ref, ref, ss.at[m], rs.at[m], where)

    def up_copy(m, back):
        r, j = m // slots, m % slots
        odd, s = j % 2, j // 2 + 1
        i = 3 * r + (1 - odd) * 2 * py + odd
        return slice_copy(i, (z - s + back + chips) % chips, up_ss, up_rs, m, up)

    def dn_copy(m, back):
        r, j = m // slots, m % slots
        odd, s = j % 2, j // 2 + 1
        i = 3 * r + odd * 2 * py + (1 - odd)
        return slice_copy(i, (z + s - back) % chips, dn_ss, dn_rs, m, down)

    def y_copy(m, i):
        r, j = m // slots, m % slots
        odd, s = j % 2, j // 2 + 1
        return slice_copy(3 * r + i, (z + (2 * odd - 1) * s + chips) % chips, y_ss, y_rs, m, along)

    def exchange(m, more=True):
        up_copy(m, 0).wait_recv()
        if more is True:
            up_copy(m + 2, 1).start()
        else:
            pl.when(m + 2 < count)(lambda: up_copy(m + 2, 1).start())
        dn_copy(m, 0).wait_recv()
        if more is True:
            dn_copy(m + 2, 1).start()
        else:
            pl.when(m + 2 < count)(lambda: dn_copy(m + 2, 1).start())
        y_copy(m, 2 * py).start()

    def partner_slices(r):
        @pl.loop(0, slots)
        def _(k):
            y_copy(r * slots + k, 2 - 2 * py).wait_recv()

    def row_copy(k, where):
        return remote(rows.at[0] if k < 3 else rows.at[2], rows.at[k], row_ss.at[k - 1], row_rs.at[k - 1], where)

    def gate_copy(k, where):
        return remote(gate_t.at[0] if k < 3 else gate_t.at[2], gate_t.at[k], gate_ss.at[k - 1], gate_rs.at[k - 1], where)

    def sum_copy(k, dst, ss, rs, c, where):
        at = pl.ds(c * blk, blk)
        return remote(acc.at[k, at], dst.at[at], ss.at[c], rs.at[c], where)

    loads = []
    for n, (src0, dst0, size) in enumerate(((px * excl, 0, 3), (px * excl + 3, 3, excl - 3), (2 * excl, excl, held - excl)) if excl > 3 else
                                           ((px * excl, 0, excl), (2 * excl, excl, held - excl))):
        for k, src in enumerate((wg_ref, wl_ref, wd_ref)):
            loads.append(pltpu.make_async_copy(src.at[pl.ds(src0, size)], wts.at[pl.ds(dst0, size), z, k], load_sem.at[3 * n + k]))
    hid_load = pltpu.make_async_copy(hid_ref, rows.at[0], load_sem.at[9])
    for load in loads[:3] + [hid_load] + loads[3:]:
        load.start()

    barrier = pltpu.get_barrier_semaphore()
    for peer in (up, down, sib, cross, along):
        pl.semaphore_signal(barrier, inc=1, device_id=peer, device_id_type=MESH)
    pl.semaphore_wait(barrier, 5)

    head = 3 if excl > 3 else 6
    for load in loads[:head]:
        load.wait()
    for m in range(2):
        up_copy(m, 1).start()
        dn_copy(m, 1).start()

    hid_load.wait()
    nrm = min(128, tok)

    @pl.loop(0, tok // nrm)
    def _(i):
        at = pl.ds(pl.multiple_of(i * nrm, nrm), nrm)
        values = rows[0, at, :].astype(jnp.float32)
        scale = lax.rsqrt(jnp.mean(values * values, axis=-1, keepdims=True) + EPS)
        rows[0, at, :] = (values * scale * pre_ref[...]).astype(jnp.bfloat16)

    for load in loads[head:]:
        load.wait()

    rtr = min(256, tok)

    @pl.loop(0, tok // rtr)
    def _(i):
        at = pl.ds(pl.multiple_of(i * rtr, rtr), rtr)
        logits = dot_t(router_ref[...], rows[0, at, :])
        shifted = jnp.exp(logits - jnp.max(logits, axis=0, keepdims=True))
        probs = shifted / jnp.sum(shifted, axis=0, keepdims=True)
        expert_ids = lax.broadcasted_iota(jnp.int32, (experts, rtr), 0)
        picks = choice_ref[:, at]
        chosen = expert_ids == picks[0:1, :]
        for j in range(1, picks.shape[0]):
            chosen = chosen | (expert_ids == picks[j:j + 1, :])
        gate_t[0, :, at] = jnp.where(chosen, probs, -1.0)

    @pl.loop(0, 4 * tok // nrm)
    def _(i):
        at = pl.ds(pl.multiple_of((i // 4) * nrm, nrm), nrm)
        acc[i % 4, at, :] = jnp.zeros((nrm, d_model), jnp.float32)

    for k, where in ((2, cross), (1, sib)):
        gate_copy(k, where).start()
        row_copy(k, where).start()

    def spread_gates(k):
        gates[k] = gate_t[k].T

    spread_gates(0)

    @pl.loop(0, slots)
    def _(j):
        exchange(j)

    row_copy(1, sib).wait_recv()
    gate_copy(1, sib).wait_recv()
    spread_gates(1)

    def work(i, k, rb):
        e = i + excl * (px + (1 - px) * jnp.minimum(i // excl, 1))
        at = pl.ds(pl.multiple_of(rb * blk, blk), blk)
        x = rows[k, at, :]
        lane = lax.broadcasted_iota(jnp.int32, (blk, experts), 1)
        gate = jnp.sum(jnp.where(lane == e, gates[k, at, :], 0.0), axis=1, keepdims=True)
        u = dot_t(x, wts[i, :, 0].reshape(width, d_model))
        v = dot_t(x, wts[i, :, 1].reshape(width, d_model))
        c = math.sqrt(2.0 / math.pi)
        cdf = 0.5 * (1.0 + jnp.tanh(c * (u + 0.044715 * (u * u * u))))
        a = jnp.where(gate >= 0.0, u * cdf * v, 0.0).astype(jnp.bfloat16)
        for n in range(d_model // ncol):
            cols = pl.ds(n * ncol, ncol)
            o = jnp.dot(a, wts[i, :, 2, :, cols].reshape(width, ncol), preferred_element_type=jnp.float32)
            acc[k, at, cols] += gate * o

    six = 6 * nblk

    def triple(r, q, sets):
        w = q // (2 * nblk)
        i = 3 * r + w + (1 - w) * 2 * py
        work(i, sets + (q // nblk) % 2, q % nblk)

    def run(m0, m1, blocks, block, actions=(), more=True):
        span = m1 - m0

        @pl.loop(0, span)
        def _(j):
            exchange(m0 + j, more)
            for slot, action in actions:
                pl.when(j == slot - m0)(action)

            @pl.loop((blocks * j + span - 1) // span, (blocks * (j + 1) + span - 1) // span)
            def _(q):
                block(q)

    def at_slot(r, j):
        return r * slots + j

    run(at_slot(1, 0), at_slot(2, 0), six, lambda q: triple(0, q, 0), [(at_slot(1, 4), lambda: partner_slices(0))])

    row_copy(2, cross).wait_recv()
    gate_copy(2, cross).wait_recv()
    row_copy(3, sib).start()
    gate_copy(3, sib).start()
    spread_gates(2)

    def far_rows():
        row_copy(3, sib).wait_recv()
        gate_copy(3, sib).wait_recv()
        spread_gates(3)

    run(at_slot(2, 0), at_slot(3, 0), 2 * six, lambda q: triple(1 - q // six, q % six, 2 * (q // six)),
        [(at_slot(2, 2), lambda: partner_slices(1)), (at_slot(2, 3), far_rows)])
    run(at_slot(3, 0), at_slot(4, 0), 2 * six, lambda q: triple(1 + q // six, q % six, 2), [(at_slot(3, 5), lambda: partner_slices(2))])
    early = six // 2
    run(at_slot(4, 0), at_slot(4, 2), early, lambda q: triple(2, q, 0))
    partner_slices(3)
    rest = excl - 9

    @pl.loop(0, 2 * nblk)
    def _(c):
        pl.when(c % nblk == 0)(lambda: exchange(at_slot(4, 2) + c // nblk))

        @pl.loop(0, rest)
        def _(q):
            work(9 + q, 3 - c // nblk, c % nblk)

        @pl.when(c < nblk)
        def _():
            sum_copy(3, fold_out, fold_ss, fold_rs, c, sib).start()

        @pl.when(c >= nblk)
        def _():
            at = pl.ds((c - nblk) * blk, blk)
            sum_copy(3, fold_out, fold_ss, fold_rs, c - nblk, sib).wait_recv()
            bring = pltpu.make_async_copy(fold_out.at[at], tmp, load_sem.at[9])
            bring.start()
            bring.wait()
            acc[2, at, :] += tmp[...]
            sum_copy(2, cross_out, cross_ss, cross_rs, c - nblk, cross).start()

    run(at_slot(4, 4), at_slot(5, 0), six - early, lambda q: triple(2, early + q, 0))
    run(at_slot(5, 0), at_slot(6, 0), six + early, lambda q: triple(3 + q // six, q % six, 0))
    run(at_slot(6, 0), at_slot(7, 0), six + early, lambda q: triple(4 + (q + early) // six, (q + early) % six, 0),
        [(at_slot(6, 0), lambda: partner_slices(4)), (at_slot(6, 5), lambda: partner_slices(5))], more=False)

    last = rounds - 1
    tail = 4 * nblk

    @pl.loop(0, tail)
    def _(q):
        triple(last, q, 0)

    partner_slices(last)

    @pl.loop(0, 2 * nblk)
    def _(q):
        work(3 * last + 2 - 2 * py, 1 - q // nblk, q % nblk)
        pl.when((q >= 1) & (q <= nblk))(lambda: sum_copy(1, part_out, part_ss, part_rs, q - 1, sib).start())

    own = pltpu.make_async_copy(acc.at[0], own_out, load_sem.at[9])
    own.start()

    @pl.loop(0, count)
    def _(m):
        up_copy(m, 1).wait_send()
        dn_copy(m, 1).wait_send()
        y_copy(m, 2 * py).wait_send()

    for k, where in ((1, sib), (2, cross), (3, sib)):
        row_copy(k, where).wait_send()
        gate_copy(k, where).wait_send()
    for c in range(nblk):
        sum_copy(3, fold_out, fold_ss, fold_rs, c, sib).wait_send()
        sum_copy(2, cross_out, cross_ss, cross_rs, c, cross).wait()
        sum_copy(1, part_out, part_ss, part_rs, c, sib).wait()
    own.wait()


def solution(mesh):
    side = math.isqrt(mesh.shape['dp'])
    chips = mesh.shape['wg'] // 2

    def local_block(hidden, choice, pre_scale, w_router, w_gelu, w_linear, w_down, post_scale):
        tok, d_model = hidden.shape
        experts, _, shard = w_gelu.shape
        blk = min(512, tok // 2)
        nblk = tok // blk
        excl = exclusive_experts(experts)
        held = experts - excl
        count = (held // 3) * (chips - 1)
        sums = jax.ShapeDtypeStruct((tok, d_model), jnp.float32)
        dma = pltpu.SemaphoreType.DMA
        flops = 2 * 2 * tok * experts * 3 * (chips * shard) * d_model
        own, part, cross, _ = pl.pallas_call(
            functools.partial(moe_kernel, side, chips, blk, excl),
            out_shape=(sums,) * 4,
            in_specs=[
                pl.BlockSpec(memory_space=pl.ANY),
                pl.BlockSpec(memory_space=pltpu.VMEM),
                pl.BlockSpec(memory_space=pltpu.VMEM),
                pl.BlockSpec(memory_space=pltpu.VMEM),
                pl.BlockSpec(memory_space=pl.ANY),
                pl.BlockSpec(memory_space=pl.ANY),
                pl.BlockSpec(memory_space=pl.ANY),
            ],
            out_specs=(pl.BlockSpec(memory_space=pl.ANY),) * 4,
            scratch_shapes=[
                pltpu.VMEM((held, chips, 3, shard, d_model), jnp.bfloat16),
                pltpu.VMEM((4, tok, d_model), jnp.bfloat16),
                pltpu.VMEM((4, tok, d_model), jnp.float32),
                pltpu.VMEM((4, experts, tok), jnp.float32),
                pltpu.VMEM((4, tok, experts), jnp.float32),
                pltpu.VMEM((blk, d_model), jnp.float32),
                dma((count,)), dma((count,)), dma((count,)), dma((count,)), dma((count,)), dma((count,)),
                dma((10,)),
                dma((3,)), dma((3,)), dma((3,)), dma((3,)),
                dma((nblk,)), dma((nblk,)), dma((nblk,)), dma((nblk,)), dma((nblk,)), dma((nblk,)),
            ],
            compiler_params=pltpu.CompilerParams(collective_id=0, has_side_effects=True, vmem_limit_bytes=VMEM_BYTES),
            cost_estimate=pl.CostEstimate(flops=flops, bytes_accessed=8 * experts * chips * shard * d_model, transcendentals=0),
        )(hidden, choice.T, pre_scale.reshape(1, d_model), w_router.T, jnp.swapaxes(w_gelu, 1, 2), jnp.swapaxes(w_linear, 1, 2), w_down)
        mixed = own + part + cross
        scaled = mixed * lax.rsqrt(jnp.mean(mixed * mixed, axis=-1, keepdims=True) + EPS) * post_scale
        return (hidden.astype(jnp.float32) + scaled).astype(jnp.bfloat16)

    row_spec = P(('dp', 'wg'), None)
    weight_in = P(None, None, 'wg')
    return jax.shard_map(local_block, mesh=mesh, in_specs=(row_spec, row_spec, P(), P(), weight_in, weight_in, P(None, 'wg', None), P()), out_specs=row_spec, check_vma=False)
```

time: 4080 us -> 258 us (0.06)
  waiting for transfers between devices: 3200 us -> 0 us
  local copies, waits for them, and re-layouts: 541 us -> 2.85 us
  Pallas kernels: 0 us -> 246 us
  matrix products: 222 us -> 0 us
  other arithmetic: 86.2 us -> 9.37 us
    all_gather x96 -> x0, waiting for transfers between devices: 3200 us -> none  [the longest x32 1130 us: one_expert(): linear_full = lax.all_gather(linear_part, 'wg', axis=1, tiled=True)]
    gather x11 -> x0, local copies, waits for them, and re-layouts: 395 us -> none  [the longest x1 154 us: local_block(): jnp.take(expert_out, slot_of, axis=0).reshape(tok_rows, top_k, d_model)]
    pallas_call x0 -> x1, Pallas kernels: none -> 246 us  [local_block(): pl.pallas_call(functools.partial(moe_kernel, side, chips, blk, excl), out...]
    dot_general x65 -> x0, matrix products: 222 us -> none  [the longest x32 149 us: one_expert(): return jnp.dot(hidden_act, down_full, preferred_element_type=jnp.float32)]
    dynamic_slice x96 -> x0, local copies, waits for them, and re-layouts: 141 us -> none  [local_block(): lax.map(one_expert, (dispatched, w_gelu, w_linear, w_down))]
  transfers between devices with their start and end apart: 96 -> 0, of which waited for: 96 -> 0; matrix products, arithmetic and copies ran while one was open for 4% -> 0% of each run, Pallas kernels for 0% -> 0%
where the time goes in v2:
time: 258 us
  Pallas kernels  246 us (95%)
  other arithmetic  9.37 us (4%)
  local copies, waits for them, and re-layouts  2.85 us (1%)
    pallas_call x1, Pallas kernels, local_block(): pl.pallas_call(functools.partial(moe_kernel, side, chips, blk, excl), out...  246 us
    reduce_sum x1, other arithmetic, local_block(): jnp.mean(mixed * mixed, axis=-1, keepdims=True) + EPS  5.42 us

profile of v2, /device:TPU:21, one launch (start us, length us, event | category | flops | bytes accessed | tf_op | source)
XLA Modules:
  0.0 257.8 jit_solution(1813663853200369090)
XLA Ops:
  0.0 245.5 %shard_map.82 = (f32[1024,1024]{1,0:T(8,128)}, f32[1024,1024]{1,0:T(8,128)}, f32[1024,1024]{1,0:T(8,128)}, f32[1024,1024]{1,0:T(8,128)}) custom-call(bf16[1024,1024]{1,0:T(8,128)(2,1)} %hid_ref.1, s32[8,1024]{1,0:T(8,128)} %bitcast.8, f32[1,1024]{1,0:T(1,128)} %bitcast.9, bf16[32,1024]{1,0:T(8,128)(2,1)} %bitcast.7, bf16[32,32,1024]{2,1,0:T(8,128)(2,1)} %bitcast.5, ...), custom_call_target="tpu_custom_call" | custom-call | flops 103079215104 | bytes 67108864 | tf_op jit(solution)/shard_map/pallas_call | solution.py:311
  245.5 0.0 copy-start
  245.5 0.0 copy-start.1
  245.5 0.0 copy-start.2
  245.6 0.0 copy-start.3
  245.6 5.4 %multiply_reduce_fusion = f32[1024]{0:T(1024)S(1)} fusion(f32[1024,1024]{1,0:T(8,128)} %get-tuple-element.10, f32[1024,1024]{1,0:T(8,128)} %get-tuple-element.8, f32[1024,1024]{1,0:T(8,128)} %get-tuple-element.9), kind=kLoop, calls=%fused_computation.1 | loop fusion | flops 4193280 | bytes 12587008 | tf_op jit(solution)/shard_map/reduce_sum | solution.py:340
  251.0 0.4 copy-done
  251.4 1.3 copy-done.1
  252.6 1.2 copy-done.2
  253.8 0.0 copy-done.3
  253.8 4.0 %add_convert_fusion = bf16[1024,1024]{1,0:T(8,128)(2,1)} fusion(bf16[1024,1024]{1,0:T(8,128)(2,1)} %hid_ref.1, f32[1024]{0:T(1024)S(1)} %copy-done.3, f32[1024]{0:T(1024)S(1)} %add_rsqrt_fusion, f32[1024,1024]{1,0:T(8,128)S(1)} %copy-done.2, f32[1024,1024]{1,0:T(8,128)S(1)} %copy-done, f32[1024,1024]{1,0:T(8,128)S(1)} %copy-done.1), kind=kLoop, calls=%fused_computation | loop fusion | flops 7340032 | bytes 16785408 | tf_op jit(solution)/shard_map/convert_element_type | solution.py:341
  (1 shorter events, 0.0 us)
Async XLA Ops:
  245.5 5.8 %copy-start = (f32[1024,1024]{1,0:T(8,128)S(1)}, f32[1024,1024]{1,0:T(8,128)}, u32[]{:S(2)}) copy-start(f32[1024,1024]{1,0:T(8,128)} %get-tuple-element.8) | copy-start | bytes 12582916
  245.5 7.1 %copy-start.1 = (f32[1024,1024]{1,0:T(8,128)S(1)}, f32[1024,1024]{1,0:T(8,128)}, u32[]{:S(2)}) copy-start(f32[1024,1024]{1,0:T(8,128)} %get-tuple-element.9) | copy-start | bytes 12582916
  245.5 8.3 %copy-start.2 = (f32[1024,1024]{1,0:T(8,128)S(1)}, f32[1024,1024]{1,0:T(8,128)}, u32[]{:S(2)}) copy-start(f32[1024,1024]{1,0:T(8,128)} %get-tuple-element.10) | copy-start | bytes 12582916
  245.6 8.3 %copy-start.3 = (f32[1024]{0:T(1024)S(1)}, f32[1024]{0:T(1024)}, u32[]{:S(2)}) copy-start(f32[1024]{0:T(1024)} %param.15) | copy-start | bytes 12292
